TPU v7x, 32 devices: a whole 2x2x4 slice. The times are simulated.
32 devices in a mesh: clip: 2 (over y), outer: 4 (over z), inner: 2 (over x), head: 2 (over core).
Axes of the slice: x: 2, y: 2, z: 4, core: 2. Of those that a mesh axis runs over, the one named last changes fastest.
Arguments:
- tokens: bfloat16 [2, 4096, 3072], P('clip', ('outer', 'inner', 'head')), parts along dimension 0, may hold values from -6 to 6
- shift_mod: float32 [2, 3072], P('clip'), parts along dimension 0, may hold values from -3 to 3
- scale_mod: float32 [2, 3072], P('clip'), parts along dimension 0, may hold values from -1.5 to 1.5
- gate_mod: float32 [2, 3072], P('clip'), parts along dimension 0, may hold values from 0.5 to 2
- query_weight: bfloat16 [3072, 3072], P('outer', ('inner', 'head')), may hold values from -0.109375 to 0.109375
- key_weight: bfloat16 [3072, 3072], P('outer', ('inner', 'head')), may hold values from -0.109375 to 0.109375
- value_weight: bfloat16 [3072, 3072], P('outer', ('inner', 'head')), may hold values from -0.109375 to 0.109375
- out_weight: bfloat16 [3072, 3072], P(('inner', 'head'), 'outer'), may hold values from -0.109375 to 0.109375
- query_gain: float32 [128], replicated, may hold values from 1 to 18, as said below
- key_gain: float32 [128], replicated, may hold values from 1 to 18, as said below
Outputs:
- attended: bfloat16 [2, 4096, 3072], P('clip', ('outer', 'inner', 'head')), parts along dimension 0
There are 2 independent parts, one for each index of `clip`. A program takes and returns all parts, laid end to end along the dimension named above; an argument that names none is the same for every part. Nothing has to cross between parts.
Inputs may be any that keep to these rules, and one draw needn't show every extreme that they name: `query_gain`: 128 positive scales. `key_gain`: 128 positive scales.
All inputs are finite; a program needn't handle non-finite values.
Results may differ from a plain program's by a relative error of at most 0.015.
The roundings to bfloat16 on the way count: a program that leaves them out, or rounds other values in their place, can miss the bound.
Values may be sent and summed in bfloat16 or wider, within the bound.
A program may use at most 192 MiB of HBM per device.

v0:
```python
import math
import jax
import jax.numpy as jnp
from jax import lax
from jax.sharding import PartitionSpec as P

EPSILON = 1e-06


def modulate(tokens, shift_mod, scale_mod):
    values = tokens.astype(jnp.float32)
    center = jnp.mean(values, axis=-1, keepdims=True)
    spread = jnp.mean(jnp.square(values - center), axis=-1, keepdims=True)
    normed = (values - center) / jnp.sqrt(spread + EPSILON)
    return (normed * (1.0 + scale_mod[:, None, :]) + shift_mod[:, None, :]).astype(jnp.bfloat16)


def head_norm(projected, gain_vec, head_dim):
    shaped = projected.reshape(projected.shape[:-1] + (projected.shape[-1] // head_dim, head_dim))
    mean_square = jnp.mean(jnp.square(shaped), axis=-1, keepdims=True)
    return (shaped / jnp.sqrt(mean_square + EPSILON) * gain_vec).astype(jnp.bfloat16)


def per_device(
    tokens,
    shift_mod,
    scale_mod,
    gate_mod,
    query_weight,
    key_weight,
    value_weight,
    out_weight,
    query_gain,
    key_gain,
):
    head_dim = query_gain.shape[0]
    modulated = modulate(tokens, shift_mod, scale_mod)
    gathered = lax.all_gather(modulated, ("inner", "head"), axis=1, tiled=True)
    clip_count, row_count, model_width = gathered.shape
    flattened = gathered.reshape(clip_count * row_count, model_width)
    local_cols = query_weight.shape[1]
    head_count = local_cols // head_dim
    full_query, full_key, full_value = (
        lax.all_gather(query_weight, "outer", axis=0, tiled=True),
        lax.all_gather(key_weight, "outer", axis=0, tiled=True),
        lax.all_gather(value_weight, "outer", axis=0, tiled=True),
    )
    query_proj = jnp.dot(flattened, full_query, preferred_element_type=jnp.float32)
    key_proj = jnp.dot(flattened, full_key, preferred_element_type=jnp.float32)
    value_proj = jnp.dot(flattened, full_value, preferred_element_type=jnp.float32)
    query_heads = head_norm(
        query_proj.reshape(clip_count, row_count, local_cols), query_gain, head_dim
    )
    key_send = head_norm(key_proj.reshape(clip_count, row_count, local_cols), key_gain, head_dim)
    key_send = key_send.reshape(clip_count, row_count, local_cols)
    value_send = value_proj.astype(jnp.bfloat16).reshape(clip_count, row_count, local_cols)
    root_size = math.sqrt(head_dim)
    full_out = lax.all_gather(out_weight, "outer", axis=1, tiled=True)
    running_max = jnp.full((clip_count, head_count, row_count), -1e30, jnp.float32)
    key_piece = lax.all_gather(key_send, "outer", axis=1, tiled=True)
    value_piece = lax.all_gather(value_send, "outer", axis=1, tiled=True)
    key_count = key_piece.shape[1]
    key_piece = key_piece.reshape(clip_count, key_count, head_count, head_dim)
    value_piece = value_piece.reshape(clip_count, key_count, head_count, head_dim)
    scores = (
        jnp.einsum("cqhd,ckhd->chqk", query_heads, key_piece, preferred_element_type=jnp.float32)
        / root_size
    )
    new_max = jnp.maximum(running_max, jnp.max(scores, axis=-1))
    weights = jnp.exp(scores - new_max[..., None])
    new_sum = jnp.sum(weights, axis=-1)
    new_acc = jnp.einsum(
        "chqk,ckhd->chqd",
        weights.astype(jnp.bfloat16),
        value_piece,
        preferred_element_type=jnp.float32,
    )
    head_out = new_acc / new_sum[..., None]
    mixed = (
        jnp.transpose(head_out, (0, 2, 1, 3))
        .reshape(clip_count * row_count, local_cols)
        .astype(jnp.bfloat16)
    )
    partial_value = jnp.dot(mixed, full_out, preferred_element_type=jnp.float32).reshape(
        clip_count, row_count, -1
    )
    summed = lax.psum_scatter(
        partial_value.astype(jnp.bfloat16), ("inner", "head"), scatter_dimension=1, tiled=True
    ).astype(jnp.float32)
    return (summed * gate_mod[:, None, :]).astype(jnp.bfloat16)


def solution(mesh):
    in_specs = (
        P("clip", ("outer", "inner", "head"), None),
        P("clip", None),
        P("clip", None),
        P("clip", None),
        P("outer", ("inner", "head")),
        P("outer", ("inner", "head")),
        P("outer", ("inner", "head")),
        P(("inner", "head"), "outer"),
        P(),
        P(),
    )
    out_specs = P("clip", ("outer", "inner", "head"), None)
    return jax.shard_map(
        per_device, mesh=mesh, in_specs=in_specs, out_specs=out_specs, check_vma=False
    )
```

profile of v0, /device:TPU:0, one launch (start us, length us, event | category | flops | bytes accessed | tf_op | source)
XLA Modules:
  0.0 723.6 jit_solution(17213850684140932397)
XLA Ops:
  6.5 0.0 copy-start
  6.5 0.0 copy-start.2
  6.5 0.0 copy-start.6
  6.5 0.0 copy-start.4
  6.5 0.0 all-gather.14.cloned.1.call-start
  6.6 0.7 all-gather.14.cloned.1.call-update
  7.3 0.0 all-gather.10.cloned.1.call-start
  7.3 1.7 convert_reduce_fusion
  9.0 0.0 copy-done.2
  9.0 0.6 fusion.12
  9.6 0.0 copy-done.6
  9.6 0.0 copy-done.4
  9.6 1.9 fusion.15
  11.6 0.0 all-gather.10.cloned.1.call-update
  11.6 0.0 all-gather.16.cloned.1.call-start
  11.7 0.7 all-gather.16.cloned.1.call-update
  12.3 0.0 all-gather.12.cloned.1.call-start
  12.4 0.5 all-gather.12.cloned.1.call-update
  12.9 0.0 all-gather.20.cloned.1.call-start
  13.0 0.0 copy-done
  13.0 88.1 %all-gather.14.cloned.1.call-done = bf16[3072,768]{1,0:T(8,128)(2,1)} async-done(((bf16[768,768]{1,0:T(8,128)(2,1)}), bf16[3072,768]{1,0:T(8,128)(2,1)}) %all-gather.14.cloned.1.call-update) | async-done | bytes 4718608 | tf_op jit(solution)/shard_map/all_gather | solution.py:45
  101.1 46.4 %all-gather.10.cloned.1.call-done = bf16[1,1024,3072]{2,1,0:T(8,128)(2,1)} async-done(((bf16[1,256,3072]{2,1,0:T(8,128)(2,1)}), bf16[1,1024,3072]{2,1,0:T(8,128)(2,1)}) %all-gather.10.cloned.1.call-update) | async-done | bytes 6291472 | tf_op jit(solution)/shard_map/all_gather | solution.py:38
  147.4 9.8 %fusion.27 = (f32[1024,768]{0,1:T(8,128)S(1)}, f32[1024,768]{0,1:T(8,128)}) fusion(bf16[3072,768]{1,0:T(8,128)(2,1)} %all-gather.14.cloned.1.call-done, bf16[1,1024,3072]{2,1,0:T(8,128)(2,1)} %all-gather.10.cloned.1.call-done), kind=kOutput, calls=%fused_computation.38 | convolution fusion | flops 4832624640 | bytes 17301504 | tf_op jit(solution)/shard_map/dot_general | solution.py:49
  157.2 0.3 reduce_sum.48
  157.5 3.6 fusion.17
  161.1 0.0 all-gather.20.cloned.1.call-update
  161.2 0.0 all-gather.22.cloned.1.call-start
  161.2 77.2 %all-gather.16.cloned.1.call-done = bf16[3072,768]{1,0:T(8,128)(2,1)} async-done(((bf16[768,768]{1,0:T(8,128)(2,1)}), bf16[3072,768]{1,0:T(8,128)(2,1)}) %all-gather.16.cloned.1.call-update) | async-done | bytes 4718608 | tf_op jit(solution)/shard_map/all_gather | solution.py:46
  238.4 9.4 %fusion.20 = bf16[1024,768]{1,0:T(8,128)(2,1)} fusion(bf16[3072,768]{1,0:T(8,128)(2,1)} %all-gather.16.cloned.1.call-done, bf16[1,1024,3072]{2,1,0:T(8,128)(2,1)} %all-gather.10.cloned.1.call-done), kind=kOutput, calls=%fused_computation.26 | convolution fusion | flops 4832624640 | bytes 12582912 | tf_op jit(solution)/shard_map/dot_general | solution.py:50
  247.8 0.0 all-gather.22.cloned.1.call-update
  247.8 0.0 all-gather.18.cloned.1.call-start
  247.9 0.7 all-gather.18.cloned.1.call-update
  248.6 0.2 reduce-scatter.2.cloned.1.call-start
  248.8 78.9 %all-gather.12.cloned.1.call-done = bf16[3072,768]{1,0:T(8,128)(2,1)} async-done(((bf16[768,768]{1,0:T(8,128)(2,1)}), bf16[3072,768]{1,0:T(8,128)(2,1)}) %all-gather.12.cloned.1.call-update) | async-done | bytes 4718608 | tf_op jit(solution)/shard_map/all_gather | solution.py:44
  327.7 10.3 %fusion.28 = (f32[1024,768]{0,1:T(8,128)}, f32[1024,768]{0,1:T(8,128)}) fusion(bf16[3072,768]{1,0:T(8,128)(2,1)} %all-gather.12.cloned.1.call-done, bf16[1,1024,3072]{2,1,0:T(8,128)(2,1)} %all-gather.10.cloned.1.call-done), kind=kOutput, calls=%fused_computation.39 | convolution fusion | flops 4832624640 | bytes 17301504 | tf_op jit(solution)/shard_map/dot_general | solution.py:48
  338.0 2.6 copy.14
  340.6 0.0 copy-start.3
  340.6 2.2 reduce_sum.47
  342.9 100.0 %all-gather.20.cloned.1.call-done = bf16[4096,768]{0,1:T(8,128)(2,1)} async-done(((bf16[1024,768]{0,1:T(8,128)(2,1)}), bf16[4096,768]{0,1:T(8,128)(2,1)}) %all-gather.20.cloned.1.call-update) | async-done | bytes 6291472 | tf_op jit(solution)/shard_map/all_gather | solution.py:60
  442.9 0.0 copy-done.3
  442.9 39.0 %multiply_reduce_fusion = (f32[6,1024]{1,0:T(8,128)S(1)}, f32[6,1024,4096]{2,1,0:T(8,128)}) fusion(bf16[4096,6,128]{0,2,1:T(8,128)(2,1)} %bitcast.44, f32[1024,6,128]{2,0,1:T(8,128)S(1)} %copy.14, f32[128]{0:T(128)S(1)} %copy-done.3, f32[1024,6]{0,1:T(8,128)S(1)} %add_sqrt_fusion.1), kind=kOutput, calls=%fused_computation.1 | convolution fusion | flops 6495135744 | bytes 110150144 | tf_op jit(solution)/shard_map/cqhd,ckhd->chqk/dot_general | solution.py:66
  481.9 76.0 %all-gather.22.cloned.1.call-done = bf16[4096,768]{1,0:T(8,128)(2,1)} async-done(((bf16[1024,768]{1,0:T(8,128)(2,1)}), bf16[4096,768]{1,0:T(8,128)(2,1)}) %all-gather.22.cloned.1.call-update) | async-done | bytes 6291472 | tf_op jit(solution)/shard_map/all_gather | solution.py:61
  557.9 8.8 %copy.16 = bf16[4096,768]{0,1:T(8,128)(2,1)} copy(bf16[4096,768]{1,0:T(8,128)(2,1)} %all-gather.22.cloned.1.call-done) | data formatting | bytes 12582912 | tf_op jit(solution)/shard_map/all_gather | solution.py:61
  566.6 31.5 %fusion = f32[6,1024]{1,0:T(8,128)S(1)} fusion(f32[6,1024,4096]{2,1,0:T(8,128)} %get-tuple-element.10, f32[6,1024]{1,0:T(8,128)S(1)} %broadcast_maximum_fusion), kind=kLoop, calls=%fused_computation.2 | loop fusion | flops 75491328 | bytes 100712448 | tf_op jit(solution)/shard_map/reduce_sum | solution.py:71
  598.1 35.6 %divide_convert_fusion = bf16[6,1024,128]{1,2,0:T(8,128)(2,1)S(1)} fusion(bf16[4096,6,128]{0,2,1:T(8,128)(2,1)} %bitcast.43, f32[6,1024,4096]{2,1,0:T(8,128)} %get-tuple-element.10, f32[6,1024]{1,0:T(8,128)S(1)} %broadcast_maximum_fusion, f32[6,1024]{1,0:T(8,128)S(1)} %fusion), kind=kOutput, calls=%fused_computation.24 | convolution fusion | flops 6519521280 | bytes 108576768 | tf_op jit(solution)/shard_map/chqk,ckhd->chqd/dot_general | solution.py:72
  633.7 13.3 %all-gather.18.cloned.1.call-done = bf16[768,3072]{1,0:T(8,128)(2,1)} async-done(((bf16[768,768]{1,0:T(8,128)(2,1)}), bf16[768,3072]{1,0:T(8,128)(2,1)}) %all-gather.18.cloned.1.call-update) | async-done | bytes 4718608 | tf_op jit(solution)/shard_map/all_gather | solution.py:58
  647.0 9.4 %convert_bitcast_fusion = bf16[1,1024,3072]{2,1,0:T(8,128)(2,1)} fusion(bf16[1024,768]{0,1:T(8,128)(2,1)S(1)} %bitcast.51, bf16[768,3072]{1,0:T(8,128)(2,1)} %all-gather.18.cloned.1.call-done), kind=kOutput, calls=%fused_computation.11 | convolution fusion | flops 4834983936 | bytes 12582912 | tf_op jit(solution)/shard_map/dot_general | solution.py:84
  656.4 0.0 copy-start.5
  656.4 0.0 reduce-scatter.2.cloned.1.call-update
  656.4 0.0 copy-start.1
  656.5 57.4 %reduce-scatter.2.cloned.1.call-done = bf16[1,256,3072]{2,1,0:T(8,128)(2,1)} async-done(((bf16[1,1024,3072]{2,1,0:T(8,128)(2,1)}), bf16[1,256,3072]{2,1,0:T(8,128)(2,1)}) %reduce-scatter.2.cloned.1.call-update) | async-done | bytes 1572880 | tf_op jit(solution)/shard_map/reduce_scatter | solution.py:87
  713.8 0.0 copy-done.5
  713.8 2.9 multiply_convert_fusion
  716.7 0.0 copy-done.1
  (7 shorter events, 0.1 us)
Async XLA Ops:
  6.5 6.4 copy-start
  6.5 2.5 copy-start.2
  6.5 3.1 copy-start.6
  6.5 3.1 copy-start.4
  6.5 94.5 %all-gather.14.cloned.1.call-start = ((), (), s32[]{:S(2)}) async-start(), calls=%async_computation.3 | async-start | bytes 5898240 | tf_op jit(solution)/shard_map/all_gather | solution.py:45
  7.3 140.1 %all-gather.10.cloned.1.call-start = ((), (), s32[]{:S(2)}) async-start(), calls=%async_computation.1 | async-start | bytes 7864320 | tf_op jit(solution)/shard_map/all_gather | solution.py:38
  11.6 226.8 %all-gather.16.cloned.1.call-start = ((), (), s32[]{:S(2)}) async-start(), calls=%async_computation.4 | async-start | bytes 5898240 | tf_op jit(solution)/shard_map/all_gather | solution.py:46
  12.3 315.3 %all-gather.12.cloned.1.call-start = ((), (), s32[]{:S(2)}) async-start(), calls=%async_computation.2 | async-start | bytes 5898240 | tf_op jit(solution)/shard_map/all_gather | solution.py:44
  12.9 430.0 %all-gather.20.cloned.1.call-start = ((), (), s32[]{:S(2)}) async-start(), calls=%async_computation.7 | async-start | bytes 7864320 | tf_op jit(solution)/shard_map/all_gather | solution.py:60
  161.2 396.7 %all-gather.22.cloned.1.call-start = ((), (), s32[]{:S(2)}) async-start(), calls=%async_computation.8 | async-start | bytes 7864320 | tf_op jit(solution)/shard_map/all_gather | solution.py:61
  247.8 399.2 %all-gather.18.cloned.1.call-start = ((), (), s32[]{:S(2)}) async-start(), calls=%async_computation.5 | async-start | bytes 5898240 | tf_op jit(solution)/shard_map/all_gather | solution.py:58
  248.6 465.3 %reduce-scatter.2.cloned.1.call-start = ((), (), s32[]{:S(2)}) async-start(), calls=%async_computation.6 | async-start | bytes 7864320 | tf_op jit(solution)/shard_map/reduce_scatter | solution.py:87
  340.6 102.2 %copy-start.3 = (f32[128]{0:T(128)S(1)}, f32[128]{0:T(128)}, u32[]{:S(2)}) copy-start(f32[128]{0:T(128)} %param.18) | copy-start | bytes 1540
  656.4 57.4 %copy-start.5 = (f32[1,3072]{1,0:T(1,128)S(1)}, f32[1,3072]{1,0:T(1,128)}, u32[]{:S(2)}) copy-start(f32[1,3072]{1,0:T(1,128)} %param.13) | copy-start | bytes 36868
  656.4 60.3 %copy-start.1 = (f32[128]{0:T(128)S(1)}, f32[128]{0:T(128)}, u32[]{:S(2)}) copy-start(f32[128]{0:T(128)} %param.19) | copy-start | bytes 1540
Sparse Core Ops, SparseCore 0:
  8.9 92.0 all-gather.13
  102.6 44.7 all-gather.9
  149.0 89.3 all-gather.15
  239.8 87.7 all-gather.11
  329.1 113.7 all-gather.19
  444.3 113.5 all-gather.21
  559.4 87.5 all-gather.17
  656.6 57.2 reduce-scatter.1
where the time goes:
time: 724 us
  waiting for transfers between devices  540 us (75%)
  matrix products  113 us (16%)
  other arithmetic  44.7 us (6%)
  between operations  13.6 us (2%)
  local copies, waits for them, and re-layouts  11.4 us (2%)
    all_gather x1, waiting for transfers between devices, per_device(): key_piece = lax.all_gather(key_send, 'outer', axis=1, tiled=True)  100 us
    all_gather x1, waiting for transfers between devices, per_device(): lax.all_gather(key_weight, 'outer', axis=0, tiled=True)  88.1 us
    all_gather x1, waiting for transfers between devices, per_device(): lax.all_gather(query_weight, 'outer', axis=0, tiled=True)  78.9 us
    all_gather x1, waiting for transfers between devices, per_device(): lax.all_gather(value_weight, 'outer', axis=0, tiled=True)  77.2 us
    all_gather x1, waiting for transfers between devices, per_device(): value_piece = lax.all_gather(value_send, 'outer', axis=1, tiled=True)  76 us
    reduce_scatter x1, waiting for transfers between devices, per_device(): lax.psum_scatter(partial_value.astype(jnp.bfloat16), ('inner', 'head'), s...  57.4 us
    all_gather x1, waiting for transfers between devices, per_device(): gathered = lax.all_gather(modulated, ('inner', 'head'), axis=1, tiled=True)  46.4 us
    dot_general x1, matrix products, per_device(): jnp.einsum('cqhd,ckhd->chqk', query_heads, key_piece, preferred_element_t...  39 us
  transfers between devices with their start and end apart: 8, of which 8 were waited for; matrix products, arithmetic and copies ran while one was open for 22% of the time, Pallas kernels for 0%

commit v1 on v0

--- a/solution.py
+++ b/solution.py
@@ -57,7 +57,14 @@
     root_size = math.sqrt(head_dim)
     full_out = lax.all_gather(out_weight, "outer", axis=1, tiled=True)
     running_max = jnp.full((clip_count, head_count, row_count), -1e30, jnp.float32)
-    key_piece = lax.all_gather(key_send, "outer", axis=1, tiled=True)
+    ring = [key_send]
+    for hop in range(3):
+        ring.append(lax.ppermute(ring[-1], "outer", [(dev, (dev + 1) % 4) for dev in range(4)]))
+    key_piece = jnp.roll(
+        jnp.concatenate(ring[::-1], axis=1),
+        (lax.axis_index("outer") + 1) * ring[0].shape[1],
+        axis=1,
+    )
     value_piece = lax.all_gather(value_send, "outer", axis=1, tiled=True)
     key_count = key_piece.shape[1]
     key_piece = key_piece.reshape(clip_count, key_count, head_count, head_dim)

time: 724 us -> 730 us (level)
  waiting for transfers between devices: 540 us -> 493 us
  starting transfers between devices: 0.49 us -> 42.2 us
  local copies, waits for them, and re-layouts: 11.4 us -> 22.1 us
    ppermute x0 -> x3, waiting for transfers between devices: none -> 188 us  [per_device(): lax.ppermute(ring[-1], 'outer', [(dev, (dev + 1) % 4) for dev in range(4)])]
    all_gather x1 -> x0, waiting for transfers between devices: 100 us -> none  [per_device(): key_piece = lax.all_gather(key_send, 'outer', axis=1, tiled=True)]
    all_gather x1, waiting for transfers between devices: 78.9 us -> 0.01 us  [per_device(): lax.all_gather(query_weight, 'outer', axis=0, tiled=True)]
    all_gather x1, waiting for transfers between devices: 76 us -> 0.02 us  [per_device(): value_piece = lax.all_gather(value_send, 'outer', axis=1, tiled=True)]
    ppermute x0 -> x3, starting transfers between devices: none -> 42 us  [per_device(): lax.ppermute(ring[-1], 'outer', [(dev, (dev + 1) % 4) for dev in range(4)])]
    reduce_scatter x1, waiting for transfers between devices: 57.4 us -> 89.4 us  [per_device(): lax.psum_scatter(partial_value.astype(jnp.bfloat16), ('inner', 'head'), s...]
    all_gather x1, waiting for transfers between devices: 13.3 us -> 0.02 us  [per_device(): full_out = lax.all_gather(out_weight, 'outer', axis=1, tiled=True)]
    all_gather x1, waiting for transfers between devices: 77.2 us -> 85.3 us  [per_device(): lax.all_gather(value_weight, 'outer', axis=0, tiled=True)]
  transfers between devices with their start and end apart: 8 -> 10, of which waited for: 8 -> 7; matrix products, arithmetic and copies ran while one was open for 22% -> 23% of each run, Pallas kernels for 0% -> 0%
where the time goes in v1:
time: 730 us
  waiting for transfers between devices  493 us (68%)
  matrix products  113 us (15%)
  other arithmetic  46 us (6%)
  starting transfers between devices  42.2 us (6%)
  local copies, waits for them, and re-layouts  22.1 us (3%)
  between operations  13.7 us (2%)
    ppermute x3, waiting for transfers between devices, per_device(): lax.ppermute(ring[-1], 'outer', [(dev, (dev + 1) % 4) for dev in range(4)])  188 us
    reduce_scatter x1, waiting for transfers between devices, per_device(): lax.psum_scatter(partial_value.astype(jnp.bfloat16), ('inner', 'head'), s...  89.4 us
    all_gather x1, waiting for transfers between devices, per_device(): lax.all_gather(value_weight, 'outer', axis=0, tiled=True)  85.3 us
    all_gather x1, waiting for transfers between devices, per_device(): lax.all_gather(key_weight, 'outer', axis=0, tiled=True)  81.5 us
    all_gather x1, waiting for transfers between devices, per_device(): gathered = lax.all_gather(modulated, ('inner', 'head'), axis=1, tiled=True)  46.4 us
    ppermute x3, starting transfers between devices, per_device(): lax.ppermute(ring[-1], 'outer', [(dev, (dev + 1) % 4) for dev in range(4)])  42 us
    dot_general x1, matrix products, per_device(): jnp.einsum('cqhd,ckhd->chqk', query_heads, key_piece, preferred_element_t...  38.7 us
    dot_general x1, matrix products, per_device(): jnp.einsum('chqk,ckhd->chqd', weights.astype(jnp.bfloat16), value_piece,...  35.3 us
  transfers between devices with their start and end apart: 10, of which 7 were waited for; matrix products, arithmetic and copies ran while one was open for 23% of the time, Pallas kernels for 0%

profile of v1, /device:TPU:0, one launch (start us, length us, event | category | flops | bytes accessed | tf_op | source)
XLA Modules:
  0.0 729.7 jit_solution(14159863932915718971)
XLA Ops:
  6.5 0.0 copy-start
  6.5 0.0 copy-start.2
  6.5 0.0 all-gather.14.cloned.1.call-start
  6.5 0.7 all-gather.14.cloned.1.call-update
  7.3 0.0 all-gather.8.cloned.1.call-start
  7.3 1.7 convert_reduce_fusion
  9.0 2.0 fusion.12
  11.0 0.7 broadcast_add_fusion
  11.7 0.0 copy-done.2
  11.7 2.6 fusion.15
  14.4 0.0 all-gather.8.cloned.1.call-update
  14.4 0.0 all-gather.12.cloned.1.call-start
  14.4 0.7 all-gather.12.cloned.1.call-update
  15.1 0.0 all-gather.10.cloned.1.call-start
  15.2 0.5 all-gather.10.cloned.1.call-update
  15.7 0.0 all-gather.18.cloned.1.call-start
  15.8 85.3 %all-gather.14.cloned.1.call-done = bf16[3072,768]{1,0:T(8,128)(2,1)} async-done(((bf16[768,768]{1,0:T(8,128)(2,1)}), bf16[3072,768]{1,0:T(8,128)(2,1)}) %all-gather.14.cloned.1.call-update) | async-done | bytes 4718608 | tf_op jit(solution)/shard_map/all_gather | solution.py:46
  101.0 46.4 %all-gather.8.cloned.1.call-done = bf16[1,1024,3072]{2,1,0:T(8,128)(2,1)} async-done(((bf16[1,256,3072]{2,1,0:T(8,128)(2,1)}), bf16[1,1024,3072]{2,1,0:T(8,128)(2,1)}) %all-gather.8.cloned.1.call-update) | async-done | bytes 6291472 | tf_op jit(solution)/shard_map/all_gather | solution.py:38
  147.4 9.4 %fusion.20 = bf16[1024,768]{1,0:T(8,128)(2,1)} fusion(bf16[3072,768]{1,0:T(8,128)(2,1)} %all-gather.14.cloned.1.call-done, bf16[1,1024,3072]{2,1,0:T(8,128)(2,1)} %all-gather.8.cloned.1.call-done), kind=kOutput, calls=%fused_computation.26 | convolution fusion | flops 4832624640 | bytes 12582912 | tf_op jit(solution)/shard_map/dot_general | solution.py:50
  156.8 0.0 all-gather.18.cloned.1.call-update
  156.8 0.0 all-gather.16.cloned.1.call-start
  156.9 0.0 copy-done
  156.9 81.5 %all-gather.12.cloned.1.call-done = bf16[3072,768]{1,0:T(8,128)(2,1)} async-done(((bf16[768,768]{1,0:T(8,128)(2,1)}), bf16[3072,768]{1,0:T(8,128)(2,1)}) %all-gather.12.cloned.1.call-update) | async-done | bytes 4718608 | tf_op jit(solution)/shard_map/all_gather | solution.py:45
  238.4 9.8 %fusion.27 = (f32[1024,768]{0,1:T(8,128)S(1)}, f32[1024,768]{0,1:T(8,128)}) fusion(bf16[3072,768]{1,0:T(8,128)(2,1)} %all-gather.12.cloned.1.call-done, bf16[1,1024,3072]{2,1,0:T(8,128)(2,1)} %all-gather.8.cloned.1.call-done), kind=kOutput, calls=%fused_computation.47 | convolution fusion | flops 4832624640 | bytes 17301504 | tf_op jit(solution)/shard_map/dot_general | solution.py:49
  248.3 0.3 reduce_sum.48
  248.6 2.3 fusion.17
  250.9 0.1 collective-permute-start
  250.9 72.4 %collective-permute-done = bf16[1,1024,768]{1,2,0:T(8,128)(2,1)S(1)} collective-permute-done((bf16[1,1024,768]{1,2,0:T(8,128)(2,1)S(1)}, bf16[1,1024,768]{1,2,0:T(8,128)(2,1)S(1)}, u32[]{:S(2)}, u32[]{:S(2)}) %collective-permute-start) | collective-permute-done | bytes 1572896 | tf_op jit(solution)/shard_map/ppermute | solution.py:62
  323.4 28.8 %collective-permute-start.1 = (bf16[1,1024,768]{1,2,0:T(8,128)(2,1)S(1)}, bf16[1,1024,768]{1,2,0:T(8,128)(2,1)}, u32[]{:S(2)}, u32[]{:S(2)}) collective-permute-start(bf16[1,1024,768]{1,2,0:T(8,128)(2,1)S(1)} %collective-permute-done), channel_id=1, source_target_pairs={{0,4},{4,8},{8,12},{12,0},{1,5},{5,9},{9,13},{13,1},{2,6},{6,10},{... | collective-permute-start | bytes 4718600 | tf_op jit(solution)/shard_map/ppermute | solution.py:62
  352.2 0.0 all-gather.16.cloned.1.call-update
  352.2 0.0 reduce-scatter.2.cloned.1.call-start
  352.3 59.6 %collective-permute-done.1 = bf16[1,1024,768]{1,2,0:T(8,128)(2,1)} collective-permute-done((bf16[1,1024,768]{1,2,0:T(8,128)(2,1)S(1)}, bf16[1,1024,768]{1,2,0:T(8,128)(2,1)}, u32[]{:S(2)}, u32[]{:S(2)}) %collective-permute-start.1) | collective-permute-done | bytes 1572896 | tf_op jit(solution)/shard_map/ppermute | solution.py:62
  411.9 13.1 %collective-permute-start.2 = (bf16[1,1024,768]{1,2,0:T(8,128)(2,1)}, bf16[1,1024,768]{1,2,0:T(8,128)(2,1)}, u32[]{:S(2)}, u32[]{:S(2)}) collective-permute-start(bf16[1,1024,768]{1,2,0:T(8,128)(2,1)} %collective-permute-done.1), channel_id=1, source_target_pairs={{0,4},{4,8},{8,12},{12,0},{1,5},{5,9},{9,13},{13,1},{2,6},{6,10},{... | collective-permute-start | bytes 4718600 | tf_op jit(solution)/shard_map/ppermute | solution.py:62
  425.0 0.0 all-gather.10.cloned.1.call-done
  425.0 10.3 %fusion.28 = (f32[1024,768]{0,1:T(8,128)}, f32[1024,768]{0,1:T(8,128)}) fusion(bf16[3072,768]{1,0:T(8,128)(2,1)} %all-gather.10.cloned.1.call-done, bf16[1,1024,3072]{2,1,0:T(8,128)(2,1)} %all-gather.8.cloned.1.call-done), kind=kOutput, calls=%fused_computation.48 | convolution fusion | flops 4832624640 | bytes 17301504 | tf_op jit(solution)/shard_map/dot_general | solution.py:48
  435.3 3.5 copy.13
  438.8 2.3 reduce_sum.47
  441.1 56.1 %collective-permute-done.2 = bf16[1,1024,768]{1,2,0:T(8,128)(2,1)} collective-permute-done((bf16[1,1024,768]{1,2,0:T(8,128)(2,1)}, bf16[1,1024,768]{1,2,0:T(8,128)(2,1)}, u32[]{:S(2)}, u32[]{:S(2)}) %collective-permute-start.2) | collective-permute-done | bytes 1572896 | tf_op jit(solution)/shard_map/ppermute | solution.py:62
  497.2 1.5 constant_dynamic-update-slice_fusion.7
  498.7 1.5 constant_dynamic-update-slice_fusion.6
  500.3 0.1 constant_dynamic-update-slice_fusion.5
  500.4 0.1 constant_dynamic-update-slice_fusion.4
  500.5 1.5 constant_dynamic-update-slice_fusion.3
  502.1 1.5 constant_dynamic-update-slice_fusion.2
  503.6 0.1 constant_dynamic-update-slice_fusion.1
  503.7 0.1 constant_dynamic-update-slice_fusion
  503.9 0.0 copy-start.3
  503.9 0.0 copy-start.4
  503.9 3.1 constant_dynamic-slice_fusion
  507.0 0.0 copy-done.3
  507.0 0.0 copy-done.4
  507.0 38.7 %multiply_reduce_fusion = (f32[6,1024]{1,0:T(8,128)S(1)}, f32[6,1024,4096]{2,1,0:T(8,128)}) fusion(bf16[4096,6,128]{0,2,1:T(8,128)(2,1)} %bitcast.46, f32[1024,6,128]{2,0,1:T(8,128)S(1)} %copy-done.3, f32[128]{0:T(128)S(1)} %copy-done.4, f32[1024,6]{0,1:T(8,128)S(1)} %add_sqrt_fusion.1), kind=kOutput, calls=%fused_computation.1 | convolution fusion | flops 6495135744 | bytes 110150144 | tf_op jit(solution)/shard_map/cqhd,ckhd->chqk/dot_general | solution.py:73
  545.7 31.2 %fusion = f32[6,1024]{1,0:T(8,128)S(1)} fusion(f32[6,1024,4096]{2,1,0:T(8,128)} %get-tuple-element.10, f32[6,1024]{1,0:T(8,128)S(1)} %broadcast_maximum_fusion), kind=kLoop, calls=%fused_computation.2 | loop fusion | flops 75491328 | bytes 100712448 | tf_op jit(solution)/shard_map/reduce_sum | solution.py:78
  576.9 0.0 all-gather.18.cloned.1.call-done
  577.0 8.9 %copy.15 = bf16[4096,768]{0,1:T(8,128)(2,1)} copy(bf16[4096,768]{1,0:T(8,128)(2,1)} %all-gather.18.cloned.1.call-done) | data formatting | bytes 12582912 | tf_op jit(solution)/shard_map/all_gather | solution.py:68
  585.8 35.3 %divide_convert_fusion = bf16[6,1024,128]{1,2,0:T(8,128)(2,1)S(1)} fusion(bf16[4096,6,128]{0,2,1:T(8,128)(2,1)} %bitcast.48, f32[6,1024,4096]{2,1,0:T(8,128)} %get-tuple-element.10, f32[6,1024]{1,0:T(8,128)S(1)} %broadcast_maximum_fusion, f32[6,1024]{1,0:T(8,128)S(1)} %fusion), kind=kOutput, calls=%fused_computation.24 | convolution fusion | flops 6519521280 | bytes 108576768 | tf_op jit(solution)/shard_map/chqk,ckhd->chqd/dot_general | solution.py:79
  621.1 0.0 all-gather.16.cloned.1.call-done
  621.1 9.4 %convert_bitcast_fusion = bf16[1,1024,3072]{2,1,0:T(8,128)(2,1)} fusion(bf16[1024,768]{0,1:T(8,128)(2,1)S(1)} %bitcast.55, bf16[768,3072]{1,0:T(8,128)(2,1)} %all-gather.16.cloned.1.call-done), kind=kOutput, calls=%fused_computation.11 | convolution fusion | flops 4834983936 | bytes 12582912 | tf_op jit(solution)/shard_map/dot_general | solution.py:91
  630.5 0.0 copy-start.5
  630.5 0.0 reduce-scatter.2.cloned.1.call-update
  630.6 89.4 %reduce-scatter.2.cloned.1.call-done = bf16[1,256,3072]{2,1,0:T(8,128)(2,1)} async-done(((bf16[1,1024,3072]{2,1,0:T(8,128)(2,1)}), bf16[1,256,3072]{2,1,0:T(8,128)(2,1)}) %reduce-scatter.2.cloned.1.call-update) | async-done | bytes 1572880 | tf_op jit(solution)/shard_map/reduce_scatter | solution.py:94
  719.9 0.0 copy-done.5
  719.9 2.9 multiply_convert_fusion
  722.9 0.0 copy-done.1
  (7 shorter events, 0.1 us)
Async XLA Ops:
  6.5 150.3 %copy-start = (f32[128]{0:T(128)S(1)}, f32[128]{0:T(128)}, u32[]{:S(2)}) copy-start(f32[128]{0:T(128)} %param.19) | copy-start | bytes 1540
  6.5 5.2 copy-start.2
  6.5 94.5 %all-gather.14.cloned.1.call-start = ((), (), s32[]{:S(2)}) async-start(), calls=%async_computation.4 | async-start | bytes 5898240 | tf_op jit(solution)/shard_map/all_gather | solution.py:46
  7.3 140.1 %all-gather.8.cloned.1.call-start = ((), (), s32[]{:S(2)}) async-start(), calls=%async_computation.1 | async-start | bytes 7864320 | tf_op jit(solution)/shard_map/all_gather | solution.py:38
  14.4 224.0 %all-gather.12.cloned.1.call-start = ((), (), s32[]{:S(2)}) async-start(), calls=%async_computation.3 | async-start | bytes 5898240 | tf_op jit(solution)/shard_map/all_gather | solution.py:45
  15.1 409.8 %all-gather.10.cloned.1.call-start = ((), (), s32[]{:S(2)}) async-start(), calls=%async_computation.2 | async-start | bytes 5898240 | tf_op jit(solution)/shard_map/all_gather | solution.py:44
  15.7 561.2 %all-gather.18.cloned.1.call-start = ((), (), s32[]{:S(2)}) async-start(), calls=%async_computation.7 | async-start | bytes 7864320 | tf_op jit(solution)/shard_map/all_gather | solution.py:68
  156.8 464.3 %all-gather.16.cloned.1.call-start = ((), (), s32[]{:S(2)}) async-start(), calls=%async_computation.5 | async-start | bytes 5898240 | tf_op jit(solution)/shard_map/all_gather | solution.py:58
  250.9 72.5 %collective-permute-start = (bf16[1,1024,768]{1,2,0:T(8,128)(2,1)S(1)}, bf16[1,1024,768]{1,2,0:T(8,128)(2,1)S(1)}, u32[]{:S(2)}, u32[]{:S(2)}) collective-permute-start(bf16[1,1024,768]{1,2,0:T(8,128)(2,1)S(1)} %bitcast.47), channel_id=1, source_target_pairs={{0,4},{4,8},{8,12},{12,0},{1,5},{5,9},{9,13},{13,1},{2,6},{6,10},{... | collective-permute-start | bytes 4718600 | tf_op jit(solution)/shard_map/ppermute | solution.py:62
  323.4 88.5 %collective-permute-start.1 = (bf16[1,1024,768]{1,2,0:T(8,128)(2,1)S(1)}, bf16[1,1024,768]{1,2,0:T(8,128)(2,1)}, u32[]{:S(2)}, u32[]{:S(2)}) collective-permute-start(bf16[1,1024,768]{1,2,0:T(8,128)(2,1)S(1)} %collective-permute-done), channel_id=1, source_target_pairs={{0,4},{4,8},{8,12},{12,0},{1,5},{5,9},{9,13},{13,1},{2,6},{6,10},{... | collective-permute-start | bytes 4718600 | tf_op jit(solution)/shard_map/ppermute | solution.py:62
  352.2 367.7 %reduce-scatter.2.cloned.1.call-start = ((), (), s32[]{:S(2)}) async-start(), calls=%async_computation.6 | async-start | bytes 7864320 | tf_op jit(solution)/shard_map/reduce_scatter | solution.py:94
  411.9 85.3 %collective-permute-start.2 = (bf16[1,1024,768]{1,2,0:T(8,128)(2,1)}, bf16[1,1024,768]{1,2,0:T(8,128)(2,1)}, u32[]{:S(2)}, u32[]{:S(2)}) collective-permute-start(bf16[1,1024,768]{1,2,0:T(8,128)(2,1)} %collective-permute-done.1), channel_id=1, source_target_pairs={{0,4},{4,8},{8,12},{12,0},{1,5},{5,9},{9,13},{13,1},{2,6},{6,10},{... | collective-permute-start | bytes 4718600 | tf_op jit(solution)/shard_map/ppermute | solution.py:62
  503.9 3.1 copy-start.3
  503.9 3.1 copy-start.4
  630.5 89.4 %copy-start.5 = (f32[1,3072]{1,0:T(1,128)S(1)}, f32[1,3072]{1,0:T(1,128)}, u32[]{:S(2)}) copy-start(f32[1,3072]{1,0:T(1,128)} %param.13) | copy-start | bytes 36868
  630.5 92.3 %copy-start.1 = (f32[128]{0:T(128)S(1)}, f32[128]{0:T(128)}, u32[]{:S(2)}) copy-start(f32[128]{0:T(128)} %param.19) | copy-start | bytes 1540
Sparse Core Ops, SparseCore 0:
  8.9 92.1 all-gather.13
  102.6 44.7 all-gather.7
  149.0 89.3 all-gather.11
  239.8 123.5 all-gather.9
  364.8 165.2 all-gather.17
  531.6 87.5 all-gather.15
  630.7 89.2 reduce-scatter.1
